TPU v7x, 256 devices: a whole 4x4x8 slice. The times are simulated.
256 devices in a mesh: px: 4 (over x_lo, core), py: 8 (over y, x_hi), pz: 8 (over z).
Axes of the slice: x: 4 (x_hi: 2, x_lo: 2; x = x_hi * 2 + x_lo), y: 4, z: 8, core: 2. Of those that a mesh axis runs over, the one named last changes fastest.
Arguments:
- control_values: float32 [28, 56, 56, 512], P('px', 'py', 'pz'), may hold values from -6 to 6
- metric_diag: float32 [3, 32, 4096], P(None, 'px', ('py', 'pz')), may hold values from 0.5 to 2
- metric_off: float32 [3, 32, 4096], P(None, 'px', ('py', 'pz')), may hold values from -0.2 to 0.2
- mass_weight: float32 [32, 4096], P('px', ('py', 'pz')), may hold values from 0.5 to 2
- orient: int32 [4, 8, 8, 3], P('px', 'py', 'pz'), may hold values from 0 to 1
Outputs:
- stiffness_out: float32 [28, 56, 56, 512], P('px', 'py', 'pz')
- mass_out: float32 [28, 56, 56, 512], P('px', 'py', 'pz')
All inputs are finite; a program needn't handle non-finite values.
Results may differ from a plain program's by a relative error of at most 0.0003.
Values sent between devices are 32-bit elements; how exact they have to be, the bound alone decides.
No kernel may reach another device: no remote copies, remote signals or barrier semaphores. Data moves between devices by JAX's collectives and lax.ppermute only.
A program may use at most 64 MiB of HBM per device.

v0:
```python
import math

import jax
import jax.numpy as jnp
import numpy as np
from jax import lax
from jax.experimental import pallas as pl
from jax.experimental.pallas import tpu as pltpu
from jax.sharding import PartitionSpec as P


def spline_tables(elements):
    knot_row = np.concatenate(
        [np.zeros(3), np.arange(elements + 1) * 1.0, np.full(3, float(elements))]
    )
    offsets = np.array([0.5 - 0.5 / math.sqrt(3.0), 0.5 + 0.5 / math.sqrt(3.0)])
    points = (np.arange(elements)[:, None] + offsets[None, :]).reshape(-1)
    intervals = np.repeat(np.arange(elements), 2) + 3
    current = np.zeros((points.size, knot_row.size - 1))
    current[np.arange(points.size), intervals] = 1.0
    previous = current
    for degree in range(1, 4):
        columns = knot_row.size - 1 - degree
        updated = np.zeros((points.size, columns))
        for i in range(columns):
            lower_gap = knot_row[i + degree] - knot_row[i]
            upper_gap = knot_row[i + degree + 1] - knot_row[i + 1]
            if lower_gap > 0:
                updated[:, i] += (points - knot_row[i]) / lower_gap * current[:, i]
            if upper_gap > 0:
                updated[:, i] += (knot_row[i + degree + 1] - points) / upper_gap * current[:, i + 1]
        previous = current
        current = updated
    slopes = np.zeros(current.shape)
    for i in range(current.shape[1]):
        lower_gap = knot_row[i + 3] - knot_row[i]
        upper_gap = knot_row[i + 4] - knot_row[i + 1]
        if lower_gap > 0:
            slopes[:, i] += 3.0 / lower_gap * previous[:, i]
        if upper_gap > 0:
            slopes[:, i] -= 3.0 / upper_gap * previous[:, i + 1]
    return (current.astype(np.float32), slopes.astype(np.float32))


VALUES, SLOPES = spline_tables(4)


def split_const(table):
    high = table.astype(jnp.bfloat16)
    low = (table - high.astype(np.float64)).astype(jnp.bfloat16)
    return high, low


def plane_table(along_j, along_k):
    out = np.zeros((8, 8, 8, 8))
    out[:, :, :7, :7] = along_j.astype(np.float64)[:, None, :, None] * along_k.astype(
        np.float64
    )[None, :, None, :]
    return out.reshape(64, 64)


def forward_table():
    table = np.concatenate(
        [
            plane_table(VALUES, VALUES),
            plane_table(SLOPES, VALUES),
            plane_table(VALUES, SLOPES),
        ]
    )
    high, low = split_const(table)
    return np.concatenate([high, high, low], axis=1)


def backward_table():
    variants = []
    for flip_j in (0, 1):
        for flip_k in (0, 1):
            values_j, slopes_j = (t[:, ::-1] if flip_j else t for t in (VALUES, SLOPES))
            values_k, slopes_k = (t[:, ::-1] if flip_k else t for t in (VALUES, SLOPES))
            plain = plane_table(values_j, values_k).T
            stiff = np.concatenate(
                [plain, plane_table(slopes_j, values_k).T, plane_table(values_j, slopes_k).T, 0 * plain],
                axis=1,
            )
            mass = np.concatenate([0 * plain] * 3 + [plain], axis=1)
            rows = [stiff, mass]
            for part in (stiff, mass):
                rows += [part[0::8], part[6::8]]
            high, low = split_const(np.concatenate(rows))
            variants.append(np.concatenate([high, low], axis=1))
    return np.stack(variants)


def accumulate(fields, metric, row, lanes, elements, sums):
    taken = {}
    for element in elements:
        active = range(element, element + 4)
        for i in active:
            if i not in taken:
                taken[i] = [fields[i, pl.ds(64 * f + row, 8), lanes] for f in range(3)]
        for q1 in (2 * element, 2 * element + 1):
            def along(table, f):
                acc = None
                for i in active:
                    term = taken[i][f] * np.float32(table[q1, i])
                    acc = term if acc is None else acc + term
                return acc

            g1, g2, g3 = along(SLOPES, 0), along(VALUES, 1), along(VALUES, 2)
            plain = along(VALUES, 0)
            d0, d1, d2, o0, o1, o2, w = (metric[8 * c + q1, pl.ds(row, 8), :] for c in range(7))
            parts = (
                (SLOPES, d0 * g1 + o0 * g2 + o1 * g3),
                (VALUES, o0 * g1 + d1 * g2 + o2 * g3),
                (VALUES, o1 * g1 + o2 * g2 + d2 * g3),
                (VALUES, w * plain),
            )
            for f, (table, flux) in enumerate(parts):
                for i in active:
                    term = flux * np.float32(table[q1, i])
                    sums[i][f] = term if sums[i][f] is None else sums[i][f] + term


def spread_metric(turned, metric, rows_of_q1):
    for c in range(7):
        for q1 in rows_of_q1:
            row = 8 * c + q1
            metric[row] = jnp.broadcast_to(turned[0:64, row : row + 1], (64, 128))


def backward_rows(table, fluxes):
    high = fluxes.astype(jnp.bfloat16)
    low = (fluxes - high.astype(jnp.float32)).astype(jnp.bfloat16)
    return (
        jnp.dot(table[:, 0:256], high, preferred_element_type=jnp.float32)
        + jnp.dot(table[:, 256:512], high, preferred_element_type=jnp.float32)
        + jnp.dot(table[:, 0:256], low, preferred_element_type=jnp.float32)
    )


OUTER, INNER = (0, 3), (1, 2)


def outer_kernel(
    u, diag, off, weight, orient, forward, backward, x_low, x_high, z_ends, fields, fluxes,
    turned, table, u_in, padded, metric, staged, small, forward_in, flags, sems,
):
    vecs = u.shape[3]
    copies = [
        pltpu.make_async_copy(orient, flags, sems.at[0]),
        pltpu.make_async_copy(diag, small.at[0:3], sems.at[1]),
        pltpu.make_async_copy(off, small.at[3:6], sems.at[2]),
        pltpu.make_async_copy(weight, small.at[6], sems.at[3]),
        pltpu.make_async_copy(forward, forward_in, sems.at[4]),
    ]
    loads = [pltpu.make_async_copy(u.at[i], u_in.at[i], sems.at[6 + i]) for i in range(7)]
    for copy in copies + loads:
        copy.start()
    padded[...] = jnp.zeros_like(padded)
    staged[...] = jnp.zeros_like(staged)
    copies[0].wait()
    flip_i, flip_j, flip_k = (flags[0, 0, 0, d] for d in range(3))
    copies.append(
        pltpu.make_async_copy(backward.at[2 * flip_j + flip_k], table, sems.at[5])
    )
    copies[5].start()
    for n in (1, 2, 3):
        copies[n].wait()
    for c in range(7):
        staged[8 * c : 8 * c + 8, 0:64] = small[c]
    turned[...] = staged[...].T
    spread_metric(turned, metric, (0, 1, 6, 7))
    copies[4].wait()

    for i in range(7):
        loads[i].wait()
        for j in range(7):
            padded[i, 8 * j : 8 * j + 7] = u_in[i, j]
        block = padded[i]
        high = block.astype(jnp.bfloat16)
        low = (block - high.astype(jnp.float32)).astype(jnp.bfloat16)
        fields[i] = jnp.dot(
            forward_in[...],
            jnp.concatenate([high, low, high], axis=0),
            preferred_element_type=jnp.float32,
        )

    def at_points(q2, carry):
        row = pl.multiple_of(q2 * 8, 8)
        for lane in range(vecs // 128):
            lanes = slice(128 * lane, 128 * lane + 128)
            sums = [[None] * 4 for _ in range(7)]
            accumulate(fields, metric, row, lanes, OUTER, sums)
            for i in range(7):
                for f in range(4):
                    fluxes[i, pl.ds(64 * f + row, 8), lanes] = sums[i][f]
        return carry

    lax.fori_loop(0, 8, at_points, 0)

    copies[5].wait()
    for side, out in enumerate((x_low, x_high)):
        rows = backward_rows(table, fluxes[jnp.where(flip_i == 1, 6 - 6 * side, 6 * side)])
        for f in range(2):
            for j in range(7):
                out[f, j] = rows[64 * f + 8 * j : 64 * f + 8 * j + 7]
        z_ends[side] = rows[128:160]


def inner_kernel(flags, fields, partial, turned, table, grid_out, z_inner, metric, fluxes):
    vecs = fields.shape[2]
    spread_metric(turned, metric, (2, 3, 4, 5))

    def at_points(q2, carry):
        row = pl.multiple_of(q2 * 8, 8)
        for lane in range(vecs // 128):
            lanes = slice(128 * lane, 128 * lane + 128)
            sums = [[None] * 4 for _ in range(7)]
            for i in range(1, 6):
                sums[i] = [partial[i, pl.ds(64 * f + row, 8), lanes] for f in range(4)]
            accumulate(fields, metric, row, lanes, INNER, sums)
            for i in range(1, 6):
                for f in range(4):
                    fluxes[i - 1, pl.ds(64 * f + row, 8), lanes] = sums[i][f]
        return carry

    lax.fori_loop(0, 8, at_points, 0)

    for spot in range(1, 6):
        rows = backward_rows(table, fluxes[jnp.where(flags[0] == 1, 6 - spot, spot) - 1])
        for f in range(2):
            for j in range(7):
                grid_out[f, spot - 1, j] = rows[64 * f + 8 * j : 64 * f + 8 * j + 7]
        z_inner[spot - 1] = rows[128:160]


def apply_outer(control_values, diag, off, weight, orient):
    vecs = control_values.shape[3]
    plane = jax.ShapeDtypeStruct((2, 7, 7, vecs), jnp.float32)
    shapes = [
        plane,
        plane,
        jax.ShapeDtypeStruct((2, 32, vecs), jnp.float32),
        jax.ShapeDtypeStruct((7, 192, vecs), jnp.float32),
        jax.ShapeDtypeStruct((7, 256, vecs), jnp.float32),
        jax.ShapeDtypeStruct((128, 128), jnp.float32),
        jax.ShapeDtypeStruct((160, 512), jnp.bfloat16),
    ]
    return pl.pallas_call(
        outer_kernel,
        out_shape=shapes,
        in_specs=[pl.BlockSpec(memory_space=pltpu.HBM)] * 7,
        scratch_shapes=[
            pltpu.VMEM((7, 7, 7, vecs), jnp.float32),
            pltpu.VMEM((7, 64, vecs), jnp.float32),
            pltpu.VMEM((56, 64, 128), jnp.float32),
            pltpu.VMEM((128, 128), jnp.float32),
            pltpu.VMEM((7, 8, 64), jnp.float32),
            pltpu.VMEM((192, 192), jnp.bfloat16),
            pltpu.SMEM((1, 1, 1, 3), jnp.int32),
            pltpu.SemaphoreType.DMA((13,)),
        ],
        compiler_params=pltpu.CompilerParams(vmem_limit_bytes=24 * 1024 * 1024),
        cost_estimate=pl.CostEstimate(flops=400_000_000, bytes_accessed=1_000_000, transcendentals=0),
        name="apply_outer",
    )(
        *(
            pltpu.with_memory_space_constraint(x, pltpu.HBM)
            for x in (
                control_values, diag, off, weight, orient,
                jnp.asarray(forward_table()), jnp.asarray(backward_table()),
            )
        )
    )


def apply_inner(flags, fields, fluxes, turned, table):
    vecs = fields.shape[2]
    return pl.pallas_call(
        inner_kernel,
        out_shape=[
            jax.ShapeDtypeStruct((2, 5, 7, 7, vecs), jnp.float32),
            jax.ShapeDtypeStruct((5, 32, vecs), jnp.float32),
        ],
        in_specs=[pl.BlockSpec(memory_space=pltpu.SMEM)] + [pl.BlockSpec(memory_space=pltpu.VMEM)] * 4,
        scratch_shapes=[
            pltpu.VMEM((56, 64, 128), jnp.float32),
            pltpu.VMEM((5, 256, vecs), jnp.float32),
        ],
        compiler_params=pltpu.CompilerParams(vmem_limit_bytes=20 * 1024 * 1024),
        cost_estimate=pl.CostEstimate(flops=400_000_000, bytes_accessed=1_000_000, transcendentals=0),
        name="apply_inner",
    )(flags, fields, fluxes, turned, table)


def small_call(kernel, shapes, *arrays, name):
    return pl.pallas_call(
        kernel,
        out_shape=shapes,
        compiler_params=pltpu.CompilerParams(vmem_limit_bytes=4 * 1024 * 1024),
        name=name,
    )(*arrays)


def planes_kernel(x_low, x_high, from_low, from_high, grid, z_ends, z_inner, y_low, y_high, z_low, z_high):
    for f in range(2):
        for end, y_out, z_out in ((0, y_low, z_low), (6, y_high, z_high)):
            group = 8 * (2 * f + (end == 6))
            for i in range(1, 6):
                y_out[f, i] = grid[f, i - 1, end]
                z_out[f, i] = z_inner[i - 1, group : group + 7]
            for side, (own, other) in enumerate(((x_low, from_low), (x_high, from_high))):
                y_out[f, 6 * side] = own[f, end] + other[f, end]
                for j in range(7):
                    z_out[f, 6 * side, j : j + 1] = (
                        z_ends[side, group + j : group + j + 1] + other[f, j, end : end + 1]
                    )


def lines_kernel(y_low, y_high, z_low, z_high):
    for end, out in ((0, z_low), (6, z_high)):
        for f in range(2):
            for side, plane in enumerate((y_low, y_high)):
                for i in range(7):
                    out[f, side, i : i + 1] = plane[f, i, end : end + 1]


def turn_source(flip_k, lanes):
    spots = lax.broadcasted_iota(jnp.int32, (8, lanes), 0)
    return jnp.where(spots < 7, jnp.where(flip_k, 6 - spots, spots), spots)


def own_block(f, i, j, grid, x_low, x_high, from_low, from_high):
    if i == 0:
        return x_low[f, j] + from_low[f, j]
    if i == 6:
        return x_high[f, j] + from_high[f, j]
    return grid[f, i - 1, j]


def turn_block(block, low_row, high_row, source):
    pad = jnp.zeros_like(low_row)
    block = jnp.concatenate([block[0:1] + low_row, block[1:6], block[6:7] + high_row, pad], axis=0)
    return jnp.take_along_axis(block, source, axis=0)[0:7]


def finish_inner_kernel(
    flags, grid, x_low, x_high, from_low, from_high, z_low, z_high, stiff, mass, ready, sems
):
    flip_i, flip_j, flip_k = (flags[d] == 1 for d in range(3))
    source = turn_source(flip_k, grid.shape[4])
    for f, out in ((0, stiff), (1, mass)):
        for i in range(7):
            for j in range(1, 6):
                block = own_block(f, i, j, grid, x_low, x_high, from_low, from_high)
                block = turn_block(block, z_low[f, i, j : j + 1], z_high[f, i, j : j + 1], source)
                ready[f, jnp.where(flip_i, 6 - i, i), jnp.where(flip_j, 6 - j, j) - 1] = block
        pltpu.make_async_copy(ready.at[f], out.at[:, 1:6], sems.at[f]).start()
    for f, out in ((0, stiff), (1, mass)):
        pltpu.make_async_copy(ready.at[f], out.at[:, 1:6], sems.at[f]).wait()


def finish_outer_kernel(
    flags, stiff_in, mass_in, grid, x_low, x_high, from_low, from_high, y_low, y_high, z_low,
    z_high, line_low, line_high, stiff, mass, ready, sems,
):
    flip_i, flip_j, flip_k = (flags[d] == 1 for d in range(3))
    source = turn_source(flip_k, grid.shape[4])
    copies = []
    for f, out in ((0, stiff), (1, mass)):
        for i in range(7):
            for side, plane in enumerate((y_low, y_high)):
                j = 6 * side
                block = own_block(f, i, j, grid, x_low, x_high, from_low, from_high) + plane[f, i]
                block = turn_block(
                    block,
                    z_low[f, i, j : j + 1] + line_low[f, side, i : i + 1],
                    z_high[f, i, j : j + 1] + line_high[f, side, i : i + 1],
                    source,
                )
                ready[f, jnp.where(flip_j, 1 - side, side), jnp.where(flip_i, 6 - i, i)] = block
        for side in range(2):
            copy = pltpu.make_async_copy(ready.at[f, side], out.at[:, 6 * side], sems.at[2 * f + side])
            copy.start()
            copies.append(copy)
    for copy in copies:
        copy.wait()


def exchange(low, high, axis):
    size = lax.axis_size(axis)
    up = [(i, (i + 1) % size) for i in range(size)]
    down = [(j, i) for i, j in up]
    return lax.ppermute(high, axis, up), lax.ppermute(low, axis, down)


def per_device(control_values, metric_diag, metric_off, mass_weight, orient):
    vecs = control_values.shape[3]
    flags = orient.reshape(3)
    out = jax.ShapeDtypeStruct((7, 7, 7, vecs), jnp.float32)
    plane = jax.ShapeDtypeStruct((2, 7, 7, vecs), jnp.float32)
    in_smem, in_vmem, in_hbm = (pl.BlockSpec(memory_space=m) for m in (pltpu.SMEM, pltpu.VMEM, pltpu.HBM))
    x_low, x_high, z_ends, fields, fluxes, turned, table = apply_outer(
        control_values, metric_diag, metric_off, mass_weight, orient
    )
    from_x = exchange(x_low, x_high, "px")
    grid, z_inner = apply_inner(flags, fields, fluxes, turned, table)
    own = (grid, x_low, x_high) + from_x
    y_low, y_high, z_low, z_high = small_call(
        planes_kernel, [plane] * 4, x_low, x_high, *from_x, grid, z_ends, z_inner, name="planes"
    )
    from_y = exchange(y_low, y_high, "py")
    from_z = exchange(z_low, z_high, "pz")
    done = pl.pallas_call(
        finish_inner_kernel,
        out_shape=[out, out],
        in_specs=[in_smem] + [in_vmem] * 7,
        out_specs=[in_hbm, in_hbm],
        scratch_shapes=[pltpu.VMEM((2, 7, 5, 7, vecs), jnp.float32), pltpu.SemaphoreType.DMA((2,))],
        compiler_params=pltpu.CompilerParams(vmem_limit_bytes=8 * 1024 * 1024),
        cost_estimate=pl.CostEstimate(flops=100_000_000, bytes_accessed=1_000_000, transcendentals=0),
        name="finish_inner",
    )(flags, *own, *from_z)
    line = jax.ShapeDtypeStruct((2, 2, 7, vecs), jnp.float32)
    from_lines = exchange(*small_call(lines_kernel, [line] * 2, *from_y, name="lines"), "pz")
    stiffness, mass = pl.pallas_call(
        finish_outer_kernel,
        out_shape=[out, out],
        in_specs=[in_smem, in_hbm, in_hbm] + [in_vmem] * 11,
        out_specs=[in_hbm, in_hbm],
        input_output_aliases={1: 0, 2: 1},
        scratch_shapes=[pltpu.VMEM((2, 2, 7, 7, vecs), jnp.float32), pltpu.SemaphoreType.DMA((4,))],
        compiler_params=pltpu.CompilerParams(vmem_limit_bytes=8 * 1024 * 1024),
        name="finish_outer",
    )(flags, *done, *own, *from_y, *from_z, *from_lines)
    return stiffness, mass


def solution(mesh):
    in_specs = (
        P("px", "py", "pz", None),
        P(None, "px", ("py", "pz")),
        P(None, "px", ("py", "pz")),
        P("px", ("py", "pz")),
        P("px", "py", "pz", None),
    )
    out_specs = (P("px", "py", "pz", None), P("px", "py", "pz", None))
    return jax.shard_map(
        per_device, mesh=mesh, in_specs=in_specs, out_specs=out_specs, check_vma=False
    )
```

profile of v0, /device:TPU:98, one launch (start us, length us, event | category | flops | bytes accessed | tf_op | source)
XLA Modules:
  0.0 38.5 jit_solution(14797786290692991980)
XLA Ops:
  0.6 4.6 %apply_outer.1 = (f32[2,7,7,512]{3,2,1,0:T(8,128)S(1)}, f32[2,7,7,512]{3,2,1,0:T(8,128)S(1)}, f32[2,32,512]{2,1,0:T(8,128)S(1)}, f32[7,192,512]{2,1,0:T(8,128)S(...) custom-call(f32[7,7,7,512]{3,2,1,0:T(8,128)} %u.1, f32[3,8,64]{2,1,0:T(8,128)} %diag.1, ...), custom_call_target="tpu_custom_call" | custom-call | flops 400000000 | bytes 1000000 | tf_op jit(solution)/shard_map/apply_outer/pallas_call | solution.py:249
  5.2 0.1 collective-permute-start.1
  5.3 0.5 %collective-permute-start = (f32[2,7,7,512]{3,2,1,0:T(8,128)S(1)}, f32[2,7,7,512]{3,2,1,0:T(8,128)S(1)}, u32[]{:S(2)}, u32[]{:S(2)}) collective-permute-start(f32[2,7,7,512]{3,2,1,0:T(8,128)S(1)} %get-tuple-element.25.x_high), channel_id=1, source_target_pairs={{0,64},{64,128},{128,192},{192,0},{1,65},{65,129},{129,193},{193,1... | collective-permute-start | bytes 602120 | tf_op jit(solution)/shard_map/ppermute | solution.py:394
  5.8 0.0 copy-start
  5.8 0.7 %copy-done = s32[1,1,1,3]{3,2,1,0:T(1,128)S(1)} copy-done((s32[1,1,1,3]{3,2,1,0:T(1,128)S(1)}, s32[1,1,1,3]{3,2,1,0:T(1,128)}, u32[]{:S(2)}) %copy-start) | copy-done | bytes 36
  6.4 3.1 %apply_inner.1 = (f32[2,5,7,7,512]{4,3,2,1,0:T(8,128)S(1)}, f32[5,32,512]{2,1,0:T(8,128)S(1)}) custom-call(s32[3]{0:T(128)S(1)} %bitcast.1, f32[7,192,512]{2,1,0:T(8,128)S(1)} %get-tuple-element.19.fields, f32[7,256,512]{2,1,0:T(8,128)S(1)} %get-tuple-element.20.partial, f32[128,128]{1,0:T(8,128)S(1)} %get-tuple-element.21.turned, ...), custom_call_target="tpu_custom_call" | custom-call | flops 400000000 | bytes 1000000 | tf_op jit(solution)/shard_map/apply_inner/pallas_call | solution.py:279
  9.6 0.8 %collective-permute-done.1.from_high = f32[2,7,7,512]{3,2,1,0:T(8,128)S(1)} collective-permute-done((f32[2,7,7,512]{3,2,1,0:T(8,128)S(1)}, f32[2,7,7,512]{3,2,1,0:T(8,128)S(1)}, u32[]{:S(2)}, u32[]{:S(2)}) %collective-permute-start.1) | collective-permute-done | bytes 200736 | tf_op jit(solution)/shard_map/ppermute | solution.py:394
  10.4 2.8 %collective-permute-done.from_low = f32[2,7,7,512]{3,2,1,0:T(8,128)S(1)} collective-permute-done((f32[2,7,7,512]{3,2,1,0:T(8,128)S(1)}, f32[2,7,7,512]{3,2,1,0:T(8,128)S(1)}, u32[]{:S(2)}, u32[]{:S(2)}) %collective-permute-start) | collective-permute-done | bytes 200736 | tf_op jit(solution)/shard_map/ppermute | solution.py:394
  13.2 0.1 planes.1
  13.3 2.2 %collective-permute-start.4 = (f32[2,7,7,512]{3,2,1,0:T(8,128)S(1)}, f32[2,7,7,512]{3,2,1,0:T(8,128)S(1)}, u32[]{:S(2)}, u32[]{:S(2)}) collective-permute-start(f32[2,7,7,512]{3,2,1,0:T(8,128)S(1)} %get-tuple-element.32), channel_id=1, source_target_pairs={{0,8},{8,16},{16,24},{24,32},{32,40},{40,48},{48,56},{56,0},{1,9},... | collective-permute-start | bytes 602120 | tf_op jit(solution)/shard_map/ppermute | solution.py:394
  15.5 3.5 %collective-permute-start.5 = (f32[2,7,7,512]{3,2,1,0:T(8,128)S(1)}, f32[2,7,7,512]{3,2,1,0:T(8,128)S(1)}, u32[]{:S(2)}, u32[]{:S(2)}) collective-permute-start(f32[2,7,7,512]{3,2,1,0:T(8,128)S(1)} %get-tuple-element.33), channel_id=1, source_target_pairs={{8,0},{16,8},{24,16},{32,24},{40,32},{48,40},{56,48},{0,56},{9,1},... | collective-permute-start | bytes 602120 | tf_op jit(solution)/shard_map/ppermute | solution.py:394
  19.0 3.1 %collective-permute-start.2 = (f32[2,7,7,512]{3,2,1,0:T(8,128)S(1)}, f32[2,7,7,512]{3,2,1,0:T(8,128)S(1)}, u32[]{:S(2)}, u32[]{:S(2)}) collective-permute-start(f32[2,7,7,512]{3,2,1,0:T(8,128)S(1)} %get-tuple-element.28), channel_id=1, source_target_pairs={{0,1},{1,2},{2,3},{3,4},{4,5},{5,6},{6,7},{7,0},{8,9},{9,10},{10,1... | collective-permute-start | bytes 602120 | tf_op jit(solution)/shard_map/ppermute | solution.py:394
  22.2 0.0 collective-permute-start.3
  22.2 3.3 %collective-permute-done.4.y_low = f32[2,7,7,512]{3,2,1,0:T(8,128)S(1)} collective-permute-done((f32[2,7,7,512]{3,2,1,0:T(8,128)S(1)}, f32[2,7,7,512]{3,2,1,0:T(8,128)S(1)}, u32[]{:S(2)}, u32[]{:S(2)}) %collective-permute-start.4) | collective-permute-done | bytes 200736 | tf_op jit(solution)/shard_map/ppermute | solution.py:394
  25.5 2.9 %collective-permute-done.5.y_high = f32[2,7,7,512]{3,2,1,0:T(8,128)S(1)} collective-permute-done((f32[2,7,7,512]{3,2,1,0:T(8,128)S(1)}, f32[2,7,7,512]{3,2,1,0:T(8,128)S(1)}, u32[]{:S(2)}, u32[]{:S(2)}) %collective-permute-start.5) | collective-permute-done | bytes 200736 | tf_op jit(solution)/shard_map/ppermute | solution.py:394
  28.4 3.2 %collective-permute-start.6 = (f32[2,2,7,512]{3,2,1,0:T(8,128)S(1)}, f32[2,2,7,512]{3,2,1,0:T(8,128)S(1)}, u32[]{:S(2)}, u32[]{:S(2)}) collective-permute-start(f32[2,2,7,512]{3,2,1,0:T(8,128)S(1)} %get-tuple-element.34), channel_id=1, source_target_pairs={{0,1},{1,2},{2,3},{3,4},{4,5},{5,6},{6,7},{7,0},{8,9},{9,10},{10,1... | collective-permute-start | bytes 172040 | tf_op jit(solution)/shard_map/ppermute | solution.py:394
  31.6 0.0 collective-permute-start.7
  31.6 0.0 collective-permute-done.2.z_low
  31.6 0.0 collective-permute-done.3.z_high
  31.6 1.7 %finish_inner.1 = (f32[7,7,7,512]{3,2,1,0:T(8,128)}, f32[7,7,7,512]{3,2,1,0:T(8,128)}) custom-call(s32[3]{0:T(128)S(1)} %bitcast.2, f32[2,5,7,7,512]{4,3,2,1,0:T(8,128)S(1)} %get-tuple-element.23.grid, f32[2,7,7,512]{3,2,1,0:T(8,128)S(1)} %get-tuple-element.24.x_low, f32[2,7,7,512]{3,2,1,0:T(8,128)S(1)} %get-tuple-element.25.x_high, ...), custom_call_target="tpu_custom_call" | custom-call | flops 100000000 | bytes 1000000 | tf_op jit(solution)/shard_map/finish_inner/pallas_call | solution.py:414
  33.4 0.2 collective-permute-done.6.line_low
  33.5 3.6 %collective-permute-done.7.line_high = f32[2,2,7,512]{3,2,1,0:T(8,128)S(1)} collective-permute-done((f32[2,2,7,512]{3,2,1,0:T(8,128)S(1)}, f32[2,2,7,512]{3,2,1,0:T(8,128)S(1)}, u32[]{:S(2)}, u32[]{:S(2)}) %collective-permute-start.7) | collective-permute-done | bytes 57376 | tf_op jit(solution)/shard_map/ppermute | solution.py:394
  37.1 1.4 %finish_outer.1 = (f32[7,7,7,512]{3,2,1,0:T(8,128)}, f32[7,7,7,512]{3,2,1,0:T(8,128)}) custom-call(s32[3]{0:T(128)S(1)} %bitcast.3, f32[7,7,7,512]{3,2,1,0:T(8,128)} %get-tuple-element.30.stiff_in, f32[7,7,7,512]{3,2,1,0:T(8,128)} %get-tuple-element.31.mass_in, ...), custom_call_target="tpu_custom_call", output_to_operand_aliasing={{0}: (1, {}), {1}: (2, {})} | custom-call | tf_op jit(solution)/shard_map/finish_outer/pallas_call | solution.py:426
  (1 shorter events, 0.0 us)
Async XLA Ops:
  5.2 5.2 %collective-permute-start.1 = (f32[2,7,7,512]{3,2,1,0:T(8,128)S(1)}, f32[2,7,7,512]{3,2,1,0:T(8,128)S(1)}, u32[]{:S(2)}, u32[]{:S(2)}) collective-permute-start(f32[2,7,7,512]{3,2,1,0:T(8,128)S(1)} %get-tuple-element.24.x_low), channel_id=1, source_target_pairs={{64,0},{128,64},{192,128},{0,192},{65,1},{129,65},{193,129},{1,193... | collective-permute-start | bytes 602120 | tf_op jit(solution)/shard_map/ppermute | solution.py:394
  5.3 7.9 %collective-permute-start = (f32[2,7,7,512]{3,2,1,0:T(8,128)S(1)}, f32[2,7,7,512]{3,2,1,0:T(8,128)S(1)}, u32[]{:S(2)}, u32[]{:S(2)}) collective-permute-start(f32[2,7,7,512]{3,2,1,0:T(8,128)S(1)} %get-tuple-element.25.x_high), channel_id=1, source_target_pairs={{0,64},{64,128},{128,192},{192,0},{1,65},{65,129},{129,193},{193,1... | collective-permute-start | bytes 602120 | tf_op jit(solution)/shard_map/ppermute | solution.py:394
  5.8 0.7 %copy-start = (s32[1,1,1,3]{3,2,1,0:T(1,128)S(1)}, s32[1,1,1,3]{3,2,1,0:T(1,128)}, u32[]{:S(2)}) copy-start(s32[1,1,1,3]{3,2,1,0:T(1,128)} %orient.1) | copy-start | bytes 40
  13.3 12.2 %collective-permute-start.4 = (f32[2,7,7,512]{3,2,1,0:T(8,128)S(1)}, f32[2,7,7,512]{3,2,1,0:T(8,128)S(1)}, u32[]{:S(2)}, u32[]{:S(2)}) collective-permute-start(f32[2,7,7,512]{3,2,1,0:T(8,128)S(1)} %get-tuple-element.32), channel_id=1, source_target_pairs={{0,8},{8,16},{16,24},{24,32},{32,40},{40,48},{48,56},{56,0},{1,9},... | collective-permute-start | bytes 602120 | tf_op jit(solution)/shard_map/ppermute | solution.py:394
  15.5 12.9 %collective-permute-start.5 = (f32[2,7,7,512]{3,2,1,0:T(8,128)S(1)}, f32[2,7,7,512]{3,2,1,0:T(8,128)S(1)}, u32[]{:S(2)}, u32[]{:S(2)}) collective-permute-start(f32[2,7,7,512]{3,2,1,0:T(8,128)S(1)} %get-tuple-element.33), channel_id=1, source_target_pairs={{8,0},{16,8},{24,16},{32,24},{40,32},{48,40},{56,48},{0,56},{9,1},... | collective-permute-start | bytes 602120 | tf_op jit(solution)/shard_map/ppermute | solution.py:394
  19.0 12.6 %collective-permute-start.2 = (f32[2,7,7,512]{3,2,1,0:T(8,128)S(1)}, f32[2,7,7,512]{3,2,1,0:T(8,128)S(1)}, u32[]{:S(2)}, u32[]{:S(2)}) collective-permute-start(f32[2,7,7,512]{3,2,1,0:T(8,128)S(1)} %get-tuple-element.28), channel_id=1, source_target_pairs={{0,1},{1,2},{2,3},{3,4},{4,5},{5,6},{6,7},{7,0},{8,9},{9,10},{10,1... | collective-permute-start | bytes 602120 | tf_op jit(solution)/shard_map/ppermute | solution.py:394
  22.2 9.5 %collective-permute-start.3 = (f32[2,7,7,512]{3,2,1,0:T(8,128)S(1)}, f32[2,7,7,512]{3,2,1,0:T(8,128)S(1)}, u32[]{:S(2)}, u32[]{:S(2)}) collective-permute-start(f32[2,7,7,512]{3,2,1,0:T(8,128)S(1)} %get-tuple-element.29), channel_id=1, source_target_pairs={{1,0},{2,1},{3,2},{4,3},{5,4},{6,5},{7,6},{0,7},{9,8},{10,9},{11,1... | collective-permute-start | bytes 602120 | tf_op jit(solution)/shard_map/ppermute | solution.py:394
  28.4 5.1 %collective-permute-start.6 = (f32[2,2,7,512]{3,2,1,0:T(8,128)S(1)}, f32[2,2,7,512]{3,2,1,0:T(8,128)S(1)}, u32[]{:S(2)}, u32[]{:S(2)}) collective-permute-start(f32[2,2,7,512]{3,2,1,0:T(8,128)S(1)} %get-tuple-element.34), channel_id=1, source_target_pairs={{0,1},{1,2},{2,3},{3,4},{4,5},{5,6},{6,7},{7,0},{8,9},{9,10},{10,1... | collective-permute-start | bytes 172040 | tf_op jit(solution)/shard_map/ppermute | solution.py:394
  31.6 5.5 %collective-permute-start.7 = (f32[2,2,7,512]{3,2,1,0:T(8,128)S(1)}, f32[2,2,7,512]{3,2,1,0:T(8,128)S(1)}, u32[]{:S(2)}, u32[]{:S(2)}) collective-permute-start(f32[2,2,7,512]{3,2,1,0:T(8,128)S(1)} %get-tuple-element.35), channel_id=1, source_target_pairs={{1,0},{2,1},{3,2},{4,3},{5,4},{6,5},{7,6},{0,7},{9,8},{10,9},{11,1... | collective-permute-start | bytes 172040 | tf_op jit(solution)/shard_map/ppermute | solution.py:394
where the time goes:
time: 38.6 us; the launch traced here: 38.5 us
  waiting for transfers between devices  13.6 us (35%)
  starting transfers between devices  12.6 us (33%)
  Pallas kernels  11 us (28%)
  between operations  0.68 us (2%)
  local copies, waits for them, and re-layouts  0.65 us (2%)
    ppermute x8, waiting for transfers between devices, exchange(): return (lax.ppermute(high, axis, up), lax.ppermute(low, axis, down))  13.6 us
    ppermute x8, starting transfers between devices, exchange(): return (lax.ppermute(high, axis, up), lax.ppermute(low, axis, down))  12.6 us
    pallas_call x1, Pallas kernels, apply_outer(): pl.pallas_call(outer_kernel, out_shape=shapes, in_specs=[pl.BlockSpec(mem...  4.56 us
    pallas_call x1, Pallas kernels, apply_inner(): pl.pallas_call(inner_kernel, out_shape=[jax.ShapeDtypeStruct((2, 5, 7, 7,...  3.13 us
    pallas_call x1, Pallas kernels, per_device(): pl.pallas_call(finish_inner_kernel, out_shape=[out, out], in_specs=[in_sm...  1.71 us
    pallas_call x1, Pallas kernels, per_device(): pl.pallas_call(finish_outer_kernel, out_shape=[out, out], in_specs=[in_sm...  1.43 us
  transfers between devices with their start and end apart: 8, of which 6 were waited for; matrix products, arithmetic and copies ran while one was open for 0% of the time, Pallas kernels for 13%

commit v1 on v0

--- a/solution.py
+++ b/solution.py
@@ -91,7 +91,7 @@
     return np.stack(variants)
 
 
-def accumulate(fields, metric, row, lanes, elements, sums):
+def accumulate(fields, metric, row, lanes, elements, wanted, sums):
     taken = {}
     for element in elements:
         active = range(element, element + 4)
@@ -116,7 +116,9 @@
                 (VALUES, w * plain),
             )
             for f, (table, flux) in enumerate(parts):
-                for i in active:
+                for i in wanted:
+                    if i not in active:
+                        continue
                     term = flux * np.float32(table[q1, i])
                     sums[i][f] = term if sums[i][f] is None else sums[i][f] + term
 
@@ -138,12 +140,33 @@
     )
 
 
-OUTER, INNER = (0, 3), (1, 2)
+def put(message, f, a, block):
+    count = block.shape[1] // 128
+    for lane in range(count):
+        message[pl.ds(count * 7 * (7 * f + a) + lane, 7, stride=count), :] = block[
+            :, 128 * lane : 128 * lane + 128
+        ]
+
+
+def get(message, f, a):
+    count = message.shape[0] // 98
+    first = count * 7 * (7 * f + a)
+    return jnp.concatenate(
+        [message[pl.ds(first + lane, 7, stride=count), :] for lane in range(count)], axis=1
+    )
+
+
+def get_row(message, f, a, b):
+    count = message.shape[0] // 98
+    first = count * (7 * (7 * f + a) + b)
+    return jnp.concatenate(
+        [message[first + lane : first + lane + 1, :] for lane in range(count)], axis=1
+    )
 
 
 def outer_kernel(
-    u, diag, off, weight, orient, forward, backward, x_low, x_high, z_ends, fields, fluxes,
-    turned, table, u_in, padded, metric, staged, small, forward_in, flags, sems,
+    u, diag, off, weight, orient, forward, backward, x_low, x_high, send_low, send_high, z_ends,
+    fields, turned, table, u_in, padded, fluxes, metric, staged, small, forward_in, flags, sems,
 ):
     vecs = u.shape[3]
     copies = [
@@ -170,10 +193,10 @@
         staged[8 * c : 8 * c + 8, 0:64] = small[c]
     turned[...] = staged[...].T
     spread_metric(turned, metric, (0, 1, 6, 7))
-    copies[4].wait()
+    for copy in copies[4:5] + loads:
+        copy.wait()
 
     for i in range(7):
-        loads[i].wait()
         for j in range(7):
             padded[i, 8 * j : 8 * j + 7] = u_in[i, j]
         block = padded[i]
@@ -190,35 +213,39 @@
         for lane in range(vecs // 128):
             lanes = slice(128 * lane, 128 * lane + 128)
             sums = [[None] * 4 for _ in range(7)]
-            accumulate(fields, metric, row, lanes, OUTER, sums)
-            for i in range(7):
+            accumulate(fields, metric, row, lanes, (0, 3), (0, 6), sums)
+            for side in range(2):
                 for f in range(4):
-                    fluxes[i, pl.ds(64 * f + row, 8), lanes] = sums[i][f]
+                    fluxes[side, pl.ds(64 * f + row, 8), lanes] = sums[6 * side][f]
         return carry
 
     lax.fori_loop(0, 8, at_points, 0)
 
     copies[5].wait()
-    for side, out in enumerate((x_low, x_high)):
-        rows = backward_rows(table, fluxes[jnp.where(flip_i == 1, 6 - 6 * side, 6 * side)])
+    for side, (out, message) in enumerate(((x_low, send_low), (x_high, send_high))):
+        rows = backward_rows(table, fluxes[jnp.where(flip_i == 1, 1 - side, side)])
         for f in range(2):
             for j in range(7):
-                out[f, j] = rows[64 * f + 8 * j : 64 * f + 8 * j + 7]
+                block = rows[64 * f + 8 * j : 64 * f + 8 * j + 7]
+                out[f, j] = block
+                put(message, f, j, block)
         z_ends[side] = rows[128:160]
 
 
-def inner_kernel(flags, fields, partial, turned, table, grid_out, z_inner, metric, fluxes):
+def inner_kernel(
+    orient, fields, turned, table, grid_out, z_inner, metric, fluxes, flags, sem
+):
     vecs = fields.shape[2]
-    spread_metric(turned, metric, (2, 3, 4, 5))
+    fetch = pltpu.make_async_copy(orient, flags, sem)
+    fetch.start()
+    spread_metric(turned, metric, range(8))
 
     def at_points(q2, carry):
         row = pl.multiple_of(q2 * 8, 8)
         for lane in range(vecs // 128):
             lanes = slice(128 * lane, 128 * lane + 128)
             sums = [[None] * 4 for _ in range(7)]
-            for i in range(1, 6):
-                sums[i] = [partial[i, pl.ds(64 * f + row, 8), lanes] for f in range(4)]
-            accumulate(fields, metric, row, lanes, INNER, sums)
+            accumulate(fields, metric, row, lanes, range(4), range(1, 6), sums)
             for i in range(1, 6):
                 for f in range(4):
                     fluxes[i - 1, pl.ds(64 * f + row, 8), lanes] = sums[i][f]
@@ -226,8 +253,10 @@
 
     lax.fori_loop(0, 8, at_points, 0)
 
+    fetch.wait()
+    flipped = flags[0, 0, 0, 0] == 1
     for spot in range(1, 6):
-        rows = backward_rows(table, fluxes[jnp.where(flags[0] == 1, 6 - spot, spot) - 1])
+        rows = backward_rows(table, fluxes[jnp.where(flipped, 6 - spot, spot) - 1])
         for f in range(2):
             for j in range(7):
                 grid_out[f, spot - 1, j] = rows[64 * f + 8 * j : 64 * f + 8 * j + 7]
@@ -237,12 +266,14 @@
 def apply_outer(control_values, diag, off, weight, orient):
     vecs = control_values.shape[3]
     plane = jax.ShapeDtypeStruct((2, 7, 7, vecs), jnp.float32)
+    message = jax.ShapeDtypeStruct((98 * vecs // 128, 128), jnp.float32)
     shapes = [
         plane,
         plane,
+        message,
+        message,
         jax.ShapeDtypeStruct((2, 32, vecs), jnp.float32),
         jax.ShapeDtypeStruct((7, 192, vecs), jnp.float32),
-        jax.ShapeDtypeStruct((7, 256, vecs), jnp.float32),
         jax.ShapeDtypeStruct((128, 128), jnp.float32),
         jax.ShapeDtypeStruct((160, 512), jnp.bfloat16),
     ]
@@ -253,6 +284,7 @@
         scratch_shapes=[
             pltpu.VMEM((7, 7, 7, vecs), jnp.float32),
             pltpu.VMEM((7, 64, vecs), jnp.float32),
+            pltpu.VMEM((2, 256, vecs), jnp.float32),
             pltpu.VMEM((56, 64, 128), jnp.float32),
             pltpu.VMEM((128, 128), jnp.float32),
             pltpu.VMEM((7, 8, 64), jnp.float32),
@@ -274,7 +306,7 @@
     )
 
 
-def apply_inner(flags, fields, fluxes, turned, table):
+def apply_inner(orient, fields, turned, table):
     vecs = fields.shape[2]
     return pl.pallas_call(
         inner_kernel,
@@ -282,15 +314,17 @@
             jax.ShapeDtypeStruct((2, 5, 7, 7, vecs), jnp.float32),
             jax.ShapeDtypeStruct((5, 32, vecs), jnp.float32),
         ],
-        in_specs=[pl.BlockSpec(memory_space=pltpu.SMEM)] + [pl.BlockSpec(memory_space=pltpu.VMEM)] * 4,
+        in_specs=[pl.BlockSpec(memory_space=pltpu.HBM)] + [pl.BlockSpec(memory_space=pltpu.VMEM)] * 3,
         scratch_shapes=[
             pltpu.VMEM((56, 64, 128), jnp.float32),
             pltpu.VMEM((5, 256, vecs), jnp.float32),
+            pltpu.SMEM((1, 1, 1, 3), jnp.int32),
+            pltpu.SemaphoreType.DMA,
         ],
         compiler_params=pltpu.CompilerParams(vmem_limit_bytes=20 * 1024 * 1024),
         cost_estimate=pl.CostEstimate(flops=400_000_000, bytes_accessed=1_000_000, transcendentals=0),
         name="apply_inner",
-    )(flags, fields, fluxes, turned, table)
+    )(pltpu.with_memory_space_constraint(orient, pltpu.HBM), fields, turned, table)
 
 
 def small_call(kernel, shapes, *arrays, name):
@@ -307,13 +341,13 @@
         for end, y_out, z_out in ((0, y_low, z_low), (6, y_high, z_high)):
             group = 8 * (2 * f + (end == 6))
             for i in range(1, 6):
-                y_out[f, i] = grid[f, i - 1, end]
+                put(y_out, f, i, grid[f, i - 1, end])
                 z_out[f, i] = z_inner[i - 1, group : group + 7]
             for side, (own, other) in enumerate(((x_low, from_low), (x_high, from_high))):
-                y_out[f, 6 * side] = own[f, end] + other[f, end]
+                put(y_out, f, 6 * side, own[f, end] + get(other, f, end))
                 for j in range(7):
                     z_out[f, 6 * side, j : j + 1] = (
-                        z_ends[side, group + j : group + j + 1] + other[f, j, end : end + 1]
+                        z_ends[side, group + j : group + j + 1] + get_row(other, f, j, end)
                     )
 
 
@@ -322,7 +356,7 @@
         for f in range(2):
             for side, plane in enumerate((y_low, y_high)):
                 for i in range(7):
-                    out[f, side, i : i + 1] = plane[f, i, end : end + 1]
+                    out[f, side, i : i + 1] = get_row(plane, f, i, end)
 
 
 def turn_source(flip_k, lanes):
@@ -332,9 +366,9 @@
 
 def own_block(f, i, j, grid, x_low, x_high, from_low, from_high):
     if i == 0:
-        return x_low[f, j] + from_low[f, j]
+        return x_low[f, j] + get(from_low, f, j)
     if i == 6:
-        return x_high[f, j] + from_high[f, j]
+        return x_high[f, j] + get(from_high, f, j)
     return grid[f, i - 1, j]
 
 
@@ -371,7 +405,8 @@
         for i in range(7):
             for side, plane in enumerate((y_low, y_high)):
                 j = 6 * side
-                block = own_block(f, i, j, grid, x_low, x_high, from_low, from_high) + plane[f, i]
+                block = own_block(f, i, j, grid, x_low, x_high, from_low, from_high)
+                block = block + get(plane, f, i)
                 block = turn_block(
                     block,
                     z_low[f, i, j : j + 1] + line_low[f, side, i : i + 1],
@@ -399,15 +434,16 @@
     flags = orient.reshape(3)
     out = jax.ShapeDtypeStruct((7, 7, 7, vecs), jnp.float32)
     plane = jax.ShapeDtypeStruct((2, 7, 7, vecs), jnp.float32)
+    message = jax.ShapeDtypeStruct((98 * vecs // 128, 128), jnp.float32)
     in_smem, in_vmem, in_hbm = (pl.BlockSpec(memory_space=m) for m in (pltpu.SMEM, pltpu.VMEM, pltpu.HBM))
-    x_low, x_high, z_ends, fields, fluxes, turned, table = apply_outer(
+    x_low, x_high, send_low, send_high, z_ends, fields, turned, table = apply_outer(
         control_values, metric_diag, metric_off, mass_weight, orient
     )
-    from_x = exchange(x_low, x_high, "px")
-    grid, z_inner = apply_inner(flags, fields, fluxes, turned, table)
+    from_x = exchange(send_low, send_high, "px")
+    grid, z_inner = apply_inner(orient, fields, turned, table)
     own = (grid, x_low, x_high) + from_x
     y_low, y_high, z_low, z_high = small_call(
-        planes_kernel, [plane] * 4, x_low, x_high, *from_x, grid, z_ends, z_inner, name="planes"
+        planes_kernel, [message] * 2 + [plane] * 2, x_low, x_high, *from_x, grid, z_ends, z_inner, name="planes"
     )
     from_y = exchange(y_low, y_high, "py")
     from_z = exchange(z_low, z_high, "pz")

time: 38.6 us -> 35.4 us (0.917)
  waiting for transfers between devices: 13.6 us -> 10 us
  starting transfers between devices: 12.6 us -> 13.9 us
  local copies, waits for them, and re-layouts: 0.65 us -> 0.01 us
    ppermute x8, waiting for transfers between devices: 13.6 us -> 10 us  [exchange(): return (lax.ppermute(high, axis, up), lax.ppermute(low, axis, down))]
    pallas_call x1, Pallas kernels: 4.56 us -> 3.3 us  [apply_outer(): pl.pallas_call(outer_kernel, out_shape=shapes, in_specs=[pl.BlockSpec(mem...]
    ppermute x8, starting transfers between devices: 12.6 us -> 13.9 us  [exchange(): return (lax.ppermute(high, axis, up), lax.ppermute(low, axis, down))]
    pallas_call x1, Pallas kernels: 3.13 us -> 3.97 us  [apply_inner(): pl.pallas_call(inner_kernel, out_shape=[jax.ShapeDtypeStruct((2, 5, 7, 7,...]
    unnamed x2, local copies, waits for them, and re-layouts: 0.65 us -> 0.01 us
  transfers between devices with their start and end apart: 8 -> 8, of which waited for: 6 -> 5; matrix products, arithmetic and copies ran while one was open for 0% -> 0% of each run, Pallas kernels for 13% -> 16%
where the time goes in v1:
time: 35.4 us; the launch traced here: 35.3 us
  starting transfers between devices  13.9 us (39%)
  Pallas kernels  10.7 us (30%)
  waiting for transfers between devices  10 us (28%)
  between operations  0.69 us (2%)
    ppermute x8, starting transfers between devices, exchange(): return (lax.ppermute(high, axis, up), lax.ppermute(low, axis, down))  13.9 us
    ppermute x8, waiting for transfers between devices, exchange(): return (lax.ppermute(high, axis, up), lax.ppermute(low, axis, down))  10 us
    pallas_call x1, Pallas kernels, apply_inner(): pl.pallas_call(inner_kernel, out_shape=[jax.ShapeDtypeStruct((2, 5, 7, 7,...  3.97 us
    pallas_call x1, Pallas kernels, apply_outer(): pl.pallas_call(outer_kernel, out_shape=shapes, in_specs=[pl.BlockSpec(mem...  3.3 us
    pallas_call x1, Pallas kernels, per_device(): pl.pallas_call(finish_inner_kernel, out_shape=[out, out], in_specs=[in_sm...  1.74 us
    pallas_call x1, Pallas kernels, per_device(): pl.pallas_call(finish_outer_kernel, out_shape=[out, out], in_specs=[in_sm...  1.44 us
  transfers between devices with their start and end apart: 8, of which 5 were waited for; matrix products, arithmetic and copies ran while one was open for 0% of the time, Pallas kernels for 16%

profile of v1, /device:TPU:98, one launch (start us, length us, event | category | flops | bytes accessed | tf_op | source)
XLA Modules:
  0.0 35.3 jit_solution(17084627551222731751)
XLA Ops:
  0.6 3.3 %apply_outer.1 = (f32[2,7,7,512]{3,2,1,0:T(8,128)S(1)}, f32[2,7,7,512]{3,2,1,0:T(8,128)S(1)}, f32[392,128]{1,0:T(8,128)S(1)}, f32[392,128]{1,0:T(8,128)S(1)}, f3...) custom-call(f32[7,7,7,512]{3,2,1,0:T(8,128)} %u.1, ...), custom_call_target="tpu_custom_call" | custom-call | flops 400000000 | bytes 1000000 | tf_op jit(solution)/shard_map/apply_outer/pallas_call | solution.py:280
  3.9 0.1 collective-permute-start
  4.0 1.7 %collective-permute-start.1 = (f32[392,128]{1,0:T(8,128)S(1)}, f32[392,128]{1,0:T(8,128)S(1)}, u32[]{:S(2)}, u32[]{:S(2)}) collective-permute-start(f32[392,128]{1,0:T(8,128)S(1)} %get-tuple-element.27), channel_id=1, source_target_pairs={{64,0},{128,64},{192,128},{0,192},{65,1},{129,65},{193,129},{1,193... | collective-permute-start | bytes 602120 | tf_op jit(solution)/shard_map/ppermute | solution.py:429
  5.8 0.0 copy-start
  5.8 4.0 %apply_inner.1 = (f32[2,5,7,7,512]{4,3,2,1,0:T(8,128)S(1)}, f32[5,32,512]{2,1,0:T(8,128)S(1)}) custom-call(s32[1,1,1,3]{3,2,1,0:T(1,128)} %orient.3, f32[7,192,512]{2,1,0:T(8,128)S(1)} %get-tuple-element.20.fields, f32[128,128]{1,0:T(8,128)S(1)} %get-tuple-element.21.turned, bf16[160,512]{1,0:T(8,128)(2,1)S(1)} %get-tuple-element.22.table), custom_call_target="tpu_custom_call" | custom-call | flops 400000000 | bytes 1000000 | tf_op jit(solution)/shard_map/apply_inner/pallas_call | solution.py:311
  9.7 0.7 %collective-permute-done.from_low = f32[392,128]{1,0:T(8,128)S(1)} collective-permute-done((f32[392,128]{1,0:T(8,128)S(1)}, f32[392,128]{1,0:T(8,128)S(1)}, u32[]{:S(2)}, u32[]{:S(2)}) %collective-permute-start) | collective-permute-done | bytes 200736 | tf_op jit(solution)/shard_map/ppermute | solution.py:429
  10.5 0.0 collective-permute-done.1.from_high
  10.5 0.2 planes.1
  10.7 1.9 %collective-permute-start.4 = (f32[392,128]{1,0:T(8,128)S(1)}, f32[392,128]{1,0:T(8,128)S(1)}, u32[]{:S(2)}, u32[]{:S(2)}) collective-permute-start(f32[392,128]{1,0:T(8,128)S(1)} %get-tuple-element.34), channel_id=1, source_target_pairs={{0,8},{8,16},{16,24},{24,32},{32,40},{40,48},{48,56},{56,0},{1,9},... | collective-permute-start | bytes 602120 | tf_op jit(solution)/shard_map/ppermute | solution.py:429
  12.6 3.8 %collective-permute-start.5 = (f32[392,128]{1,0:T(8,128)S(1)}, f32[392,128]{1,0:T(8,128)S(1)}, u32[]{:S(2)}, u32[]{:S(2)}) collective-permute-start(f32[392,128]{1,0:T(8,128)S(1)} %get-tuple-element.35), channel_id=1, source_target_pairs={{8,0},{16,8},{24,16},{32,24},{40,32},{48,40},{56,48},{0,56},{9,1},... | collective-permute-start | bytes 602120 | tf_op jit(solution)/shard_map/ppermute | solution.py:429
  16.4 3.1 %collective-permute-start.2 = (f32[2,7,7,512]{3,2,1,0:T(8,128)S(1)}, f32[2,7,7,512]{3,2,1,0:T(8,128)S(1)}, u32[]{:S(2)}, u32[]{:S(2)}) collective-permute-start(f32[2,7,7,512]{3,2,1,0:T(8,128)S(1)} %get-tuple-element.30), channel_id=1, source_target_pairs={{0,1},{1,2},{2,3},{3,4},{4,5},{5,6},{6,7},{7,0},{8,9},{9,10},{10,1... | collective-permute-start | bytes 602120 | tf_op jit(solution)/shard_map/ppermute | solution.py:429
  19.5 0.0 collective-permute-start.3
  19.5 2.7 %collective-permute-done.4.y_low = f32[392,128]{1,0:T(8,128)S(1)} collective-permute-done((f32[392,128]{1,0:T(8,128)S(1)}, f32[392,128]{1,0:T(8,128)S(1)}, u32[]{:S(2)}, u32[]{:S(2)}) %collective-permute-start.4) | collective-permute-done | bytes 200736 | tf_op jit(solution)/shard_map/ppermute | solution.py:429
  22.2 2.9 %collective-permute-done.5.y_high = f32[392,128]{1,0:T(8,128)S(1)} collective-permute-done((f32[392,128]{1,0:T(8,128)S(1)}, f32[392,128]{1,0:T(8,128)S(1)}, u32[]{:S(2)}, u32[]{:S(2)}) %collective-permute-start.5) | collective-permute-done | bytes 200736 | tf_op jit(solution)/shard_map/ppermute | solution.py:429
  25.1 0.1 lines.1
  25.2 3.2 %collective-permute-start.6 = (f32[2,2,7,512]{3,2,1,0:T(8,128)S(1)}, f32[2,2,7,512]{3,2,1,0:T(8,128)S(1)}, u32[]{:S(2)}, u32[]{:S(2)}) collective-permute-start(f32[2,2,7,512]{3,2,1,0:T(8,128)S(1)} %get-tuple-element.36), channel_id=1, source_target_pairs={{0,1},{1,2},{2,3},{3,4},{4,5},{5,6},{6,7},{7,0},{8,9},{9,10},{10,1... | collective-permute-start | bytes 172040 | tf_op jit(solution)/shard_map/ppermute | solution.py:429
  28.4 0.0 collective-permute-start.7
  28.4 0.0 collective-permute-done.2.z_low
  28.4 0.0 collective-permute-done.3.z_high
  28.4 0.0 copy-done
  28.4 1.7 %finish_inner.1 = (f32[7,7,7,512]{3,2,1,0:T(8,128)}, f32[7,7,7,512]{3,2,1,0:T(8,128)}) custom-call(s32[3]{0:T(128)S(1)} %bitcast.1, f32[2,5,7,7,512]{4,3,2,1,0:T(8,128)S(1)} %get-tuple-element.23.grid, f32[2,7,7,512]{3,2,1,0:T(8,128)S(1)} %get-tuple-element.24.x_low, f32[2,7,7,512]{3,2,1,0:T(8,128)S(1)} %get-tuple-element.25.x_high, ...), custom_call_target="tpu_custom_call" | custom-call | flops 100000000 | bytes 1000000 | tf_op jit(solution)/shard_map/finish_inner/pallas_call | solution.py:450
  30.1 0.1 collective-permute-done.6.line_low
  30.3 3.6 %collective-permute-done.7.line_high = f32[2,2,7,512]{3,2,1,0:T(8,128)S(1)} collective-permute-done((f32[2,2,7,512]{3,2,1,0:T(8,128)S(1)}, f32[2,2,7,512]{3,2,1,0:T(8,128)S(1)}, u32[]{:S(2)}, u32[]{:S(2)}) %collective-permute-start.7) | collective-permute-done | bytes 57376 | tf_op jit(solution)/shard_map/ppermute | solution.py:429
  33.8 1.4 %finish_outer.1 = (f32[7,7,7,512]{3,2,1,0:T(8,128)}, f32[7,7,7,512]{3,2,1,0:T(8,128)}) custom-call(s32[3]{0:T(128)S(1)} %bitcast.2, f32[7,7,7,512]{3,2,1,0:T(8,128)} %get-tuple-element.32.stiff_in, f32[7,7,7,512]{3,2,1,0:T(8,128)} %get-tuple-element.33.mass_in, ...), custom_call_target="tpu_custom_call", output_to_operand_aliasing={{0}: (1, {}), {1}: (2, {})} | custom-call | tf_op jit(solution)/shard_map/finish_outer/pallas_call | solution.py:462
Async XLA Ops:
  3.9 6.5 %collective-permute-start = (f32[392,128]{1,0:T(8,128)S(1)}, f32[392,128]{1,0:T(8,128)S(1)}, u32[]{:S(2)}, u32[]{:S(2)}) collective-permute-start(f32[392,128]{1,0:T(8,128)S(1)} %get-tuple-element.26), channel_id=1, source_target_pairs={{0,64},{64,128},{128,192},{192,0},{1,65},{65,129},{129,193},{193,1... | collective-permute-start | bytes 602120 | tf_op jit(solution)/shard_map/ppermute | solution.py:429
  4.0 6.5 %collective-permute-start.1 = (f32[392,128]{1,0:T(8,128)S(1)}, f32[392,128]{1,0:T(8,128)S(1)}, u32[]{:S(2)}, u32[]{:S(2)}) collective-permute-start(f32[392,128]{1,0:T(8,128)S(1)} %get-tuple-element.27), channel_id=1, source_target_pairs={{64,0},{128,64},{192,128},{0,192},{65,1},{129,65},{193,129},{1,193... | collective-permute-start | bytes 602120 | tf_op jit(solution)/shard_map/ppermute | solution.py:429
  5.8 22.6 %copy-start = (s32[1,1,1,3]{3,2,1,0:T(1,128)S(1)}, s32[1,1,1,3]{3,2,1,0:T(1,128)}, u32[]{:S(2)}) copy-start(s32[1,1,1,3]{3,2,1,0:T(1,128)} %orient.3) | copy-start | bytes 40
  10.7 11.6 %collective-permute-start.4 = (f32[392,128]{1,0:T(8,128)S(1)}, f32[392,128]{1,0:T(8,128)S(1)}, u32[]{:S(2)}, u32[]{:S(2)}) collective-permute-start(f32[392,128]{1,0:T(8,128)S(1)} %get-tuple-element.34), channel_id=1, source_target_pairs={{0,8},{8,16},{16,24},{24,32},{32,40},{40,48},{48,56},{56,0},{1,9},... | collective-permute-start | bytes 602120 | tf_op jit(solution)/shard_map/ppermute | solution.py:429
  12.6 12.5 %collective-permute-start.5 = (f32[392,128]{1,0:T(8,128)S(1)}, f32[392,128]{1,0:T(8,128)S(1)}, u32[]{:S(2)}, u32[]{:S(2)}) collective-permute-start(f32[392,128]{1,0:T(8,128)S(1)} %get-tuple-element.35), channel_id=1, source_target_pairs={{8,0},{16,8},{24,16},{32,24},{40,32},{48,40},{56,48},{0,56},{9,1},... | collective-permute-start | bytes 602120 | tf_op jit(solution)/shard_map/ppermute | solution.py:429
  16.4 12.0 %collective-permute-start.2 = (f32[2,7,7,512]{3,2,1,0:T(8,128)S(1)}, f32[2,7,7,512]{3,2,1,0:T(8,128)S(1)}, u32[]{:S(2)}, u32[]{:S(2)}) collective-permute-start(f32[2,7,7,512]{3,2,1,0:T(8,128)S(1)} %get-tuple-element.30), channel_id=1, source_target_pairs={{0,1},{1,2},{2,3},{3,4},{4,5},{5,6},{6,7},{7,0},{8,9},{9,10},{10,1... | collective-permute-start | bytes 602120 | tf_op jit(solution)/shard_map/ppermute | solution.py:429
  19.5 8.9 %collective-permute-start.3 = (f32[2,7,7,512]{3,2,1,0:T(8,128)S(1)}, f32[2,7,7,512]{3,2,1,0:T(8,128)S(1)}, u32[]{:S(2)}, u32[]{:S(2)}) collective-permute-start(f32[2,7,7,512]{3,2,1,0:T(8,128)S(1)} %get-tuple-element.31), channel_id=1, source_target_pairs={{1,0},{2,1},{3,2},{4,3},{5,4},{6,5},{7,6},{0,7},{9,8},{10,9},{11,1... | collective-permute-start | bytes 602120 | tf_op jit(solution)/shard_map/ppermute | solution.py:429
  25.2 5.1 %collective-permute-start.6 = (f32[2,2,7,512]{3,2,1,0:T(8,128)S(1)}, f32[2,2,7,512]{3,2,1,0:T(8,128)S(1)}, u32[]{:S(2)}, u32[]{:S(2)}) collective-permute-start(f32[2,2,7,512]{3,2,1,0:T(8,128)S(1)} %get-tuple-element.36), channel_id=1, source_target_pairs={{0,1},{1,2},{2,3},{3,4},{4,5},{5,6},{6,7},{7,0},{8,9},{9,10},{10,1... | collective-permute-start | bytes 172040 | tf_op jit(solution)/shard_map/ppermute | solution.py:429
  28.4 5.5 %collective-permute-start.7 = (f32[2,2,7,512]{3,2,1,0:T(8,128)S(1)}, f32[2,2,7,512]{3,2,1,0:T(8,128)S(1)}, u32[]{:S(2)}, u32[]{:S(2)}) collective-permute-start(f32[2,2,7,512]{3,2,1,0:T(8,128)S(1)} %get-tuple-element.37), channel_id=1, source_target_pairs={{1,0},{2,1},{3,2},{4,3},{5,4},{6,5},{7,6},{0,7},{9,8},{10,9},{11,1... | collective-permute-start | bytes 172040 | tf_op jit(solution)/shard_map/ppermute | solution.py:429
